TPU v7x, 256 devices: a whole 4x4x8 slice. The times are simulated.
256 devices in a mesh: row: 16 (over z, y_lo), col: 16 (over x, y_hi, core).
Axes of the slice: x: 4, y: 4 (y_hi: 2, y_lo: 2; y = y_hi * 2 + y_lo), z: 8, core: 2. Of those that a mesh axis runs over, the one named last changes fastest.
Arguments:
- matrix: float32 [12288, 12288], P('row', 'col'), may hold values from -30 to 30
- panels: float32 [2, 12288, 256], P(None, ('col', 'row')), may hold values from -0.0546875 to 0.0546875
- factors: float32 [2, 256, 256], replicated, may hold values from -1 to 2, as said below
Outputs:
- reduced: float32 [12288, 12288], P('row', 'col')
Inputs may be any that keep to these rules, and one draw needn't show every extreme that they name: Each factors[s] is upper triangular with diagonal entries between 1 and 2.
All inputs are finite; a program needn't handle non-finite values.
Results may differ from a plain program's by a relative error of at most 0.0003.
Values sent between devices are 32-bit elements; how exact they have to be, the bound alone decides.
A program may use at most 64 MiB of HBM per device.

v0:
```python
import jax
import jax.numpy as jnp
from jax import lax
from jax.sharding import PartitionSpec as P

highest = lax.Precision.HIGHEST


def laid_out(tiles, dim):
    dims = list(tiles.shape[1:])
    dims[dim] *= tiles.shape[0]
    return jnp.moveaxis(tiles, 0, dim).reshape(dims)


def from_everyone(value, axis):
    copies = jnp.broadcast_to(value, (lax.axis_size(axis), *value.shape))
    return lax.all_to_all(copies, axis, split_axis=0, concat_axis=0, tiled=True)


def gathered_copies(value, axis, dim):
    return laid_out(from_everyone(value, axis), dim)


def padded_to(lines, peers):
    spare = -len(lines) % peers
    return jnp.pad(lines, [(0, spare)] + [(0, 0)] * (lines.ndim - 1))


def broadcast_by_parts(value, axis, root):
    lines = jnp.where(lax.axis_index(axis) == root, value, jnp.zeros_like(value)).reshape(
        -1, *value.shape[1:][-1:]
    )
    padded = padded_to(lines, lax.axis_size(axis))
    own = lax.psum_scatter(padded, axis, scatter_dimension=0, tiled=True)
    return lax.all_gather(own, axis, axis=0, tiled=True)[: len(lines)].reshape(value.shape)


def cut_along(value, dim, peers):
    before, after = (value.shape[:dim], value.shape[dim + 1 :])
    return jnp.moveaxis(value.reshape(*before, peers, -1, *after), dim, 0)


def sent_and_summed(value, axis, dim):
    tiles = cut_along(value, dim, lax.axis_size(axis))
    arrived = lax.all_to_all(tiles, axis, split_axis=0, concat_axis=0, tiled=True)
    return arrived.sum(axis=0)


def nested_sum(value, axes):
    lines = value.reshape(-1, value.shape[-1])
    own = sent_and_summed(padded_to(lines, lax.axis_size(axes)), axes, 0)
    whole = gathered_copies(own, axes, 0)
    return whole[: len(lines)].reshape(value.shape)


def matmul(left, right):
    return jnp.dot(left, right, precision=highest, preferred_element_type=jnp.float32)


def transposed_product(left, right):
    return lax.dot_general(
        left, right, (((0,), (0,)), ((), ())), precision=highest, preferred_element_type=jnp.float32
    )


def outer_product(left, right):
    return lax.dot_general(
        left, right, (((1,), (1,)), ((), ())), precision=highest, preferred_element_type=jnp.float32
    )


def per_device(matrix, panels, factors):
    row_count = lax.axis_size("row")
    col_count = lax.axis_size("col")
    my_row = lax.axis_index("row")
    block_rows = matrix.shape[0]
    share = panels.shape[1]
    source = my_row * col_count // row_count
    offset = share * (my_row * col_count - source * row_count)
    gathered = gathered_copies(panels, "row", 1)
    relayed = broadcast_by_parts(gathered, "col", source)
    current = matrix
    for section in range(panels.shape[0]):
        factor = factors[section]
        panel_cols = gathered[section]
        panel_rows = relayed[section]
        sums_rows = nested_sum(matmul(current, panel_cols), "col")
        sums_cols = nested_sum(transposed_product(current, panel_rows), "row")
        image_rows = matmul(sums_rows, factor)
        image_cols = matmul(sums_cols, factor)
        inner = nested_sum(transposed_product(panel_rows, image_rows), "row")
        correction = transposed_product(factor, inner)
        update_rows = image_rows - 0.5 * matmul(panel_rows, correction)
        update_cols = image_cols - 0.5 * matmul(panel_cols, correction)
        current = (
            current
            - outer_product(panel_rows, update_cols)
            - outer_product(update_rows, panel_cols)
        )
    return current


def solution(mesh):
    return jax.shard_map(
        per_device,
        mesh=mesh,
        in_specs=(P("row", "col"), P(None, ("col", "row"), None), P()),
        out_specs=P("row", "col"),
        check_vma=False,
    )
```

profile of v0, /device:TPU:2, one launch (start us, length us, event | category | flops | bytes accessed | tf_op | source)
XLA Modules:
  0.0 431.1 jit_solution(6263676906609410572)
XLA Ops:
  8.7 9.6 %all-to-all-start = ((f32[16,2,48,256]{3,2,1,0:T(8,128)}), f32[16,2,48,256]{3,2,1,0:T(8,128)S(1)}, u32[]{:S(2)}, u32[]{:S(2)}) async-start(f32[16,2,48,256]{3,2,1,0:T(8,128)} %broadcast_in_dim.24), calls=%async_computation | async-start | bytes 3145728 | tf_op jit(solution)/shard_map/all_to_all | solution.py:17
  18.4 39.6 %all-to-all-done = f32[16,2,48,256]{3,2,1,0:T(8,128)S(1)} async-done(((f32[16,2,48,256]{3,2,1,0:T(8,128)}), f32[16,2,48,256]{3,2,1,0:T(8,128)S(1)}, u32[]{:S(2)}, u32[]{:S(2)}) %all-to-all-start) | async-done | bytes 1572896 | tf_op jit(solution)/shard_map/all_to_all | solution.py:17
  59.3 73.6 %reduce-scatter.2.cloned.1.call-done = f32[96,256]{1,0:T(8,128)} async-done(((f32[1536,256]{1,0:T(8,128)}), f32[96,256]{1,0:T(8,128)}) %reduce-scatter.2.cloned.1.call-update) | async-done | bytes 98320 | tf_op jit(solution)/shard_map/reduce_scatter | solution.py:34
  137.0 18.4 %all_to_all.65 = f32[16,48,256]{2,1,0:T(8,128)S(1)} all-to-all(f32[16,48,256]{2,1,0:T(8,128)S(1)} %fusion.38), channel_id=1, replica_groups=mesh['row'=16,'col'=16] {'col'}, dimensions={0} | all-to-all | bytes 1572864 | tf_op jit(solution)/shard_map/all_to_all | solution.py:45
  155.6 17.7 %all_to_all.66 = f32[16,48,256]{2,1,0:T(8,128)S(1)} all-to-all(f32[16,48,256]{2,1,0:T(8,128)S(1)} %broadcast_in_dim.27), channel_id=1, replica_groups=mesh['row'=16,'col'=16] {'col'}, dimensions={0} | all-to-all | bytes 1572864 | tf_op jit(solution)/shard_map/all_to_all | solution.py:17
  175.0 13.4 %all-gather.2.cloned.1.call-done = f32[1536,256]{1,0:T(8,128)} async-done(((f32[96,256]{1,0:T(8,128)}), f32[1536,256]{1,0:T(8,128)}) %all-gather.2.cloned.1.call-update) | async-done | bytes 1572880 | tf_op jit(solution)/shard_map/all_gather | solution.py:35
  188.3 3.6 fusion.16
  191.9 7.1 %all-to-all-start.5 = ((f32[16,16,256]{2,1,0:T(8,128)}), f32[16,16,256]{2,1,0:T(8,128)S(1)}, u32[]{:S(2)}, u32[]{:S(2)}) async-start(f32[16,16,256]{2,1,0:T(8,128)} %bitcast.10), calls=%async_computation.6 | async-start | bytes 524288 | tf_op jit(solution)/shard_map/all_to_all | solution.py:45
  199.1 4.7 %convolution_bitcast_fusion = f32[768,256]{0,1:T(8,128)} fusion(f32[768,768]{1,0:T(8,128)} %param.3, f32[1536,256]{1,0:T(8,128)S(1)} %copy-done), kind=kOutput, calls=%fused_computation.3 | convolution fusion | flops 1811939328 | bytes 3932160 | tf_op jit(solution)/shard_map/dot_general | solution.py:61
  203.8 2.3 copy.9
  206.1 5.4 %all-to-all-done.5 = f32[16,16,256]{2,1,0:T(8,128)S(1)} async-done(((f32[16,16,256]{2,1,0:T(8,128)}), f32[16,16,256]{2,1,0:T(8,128)S(1)}, u32[]{:S(2)}, u32[]{:S(2)}) %all-to-all-start.5) | async-done | bytes 262176 | tf_op jit(solution)/shard_map/all_to_all | solution.py:45
  211.4 4.3 all-to-all-start.1
  215.8 22.5 %all-to-all-done.1 = f32[16,48,256]{2,1,0:T(8,128)} async-done(((f32[16,48,256]{2,1,0:T(8,128)}), f32[16,48,256]{2,1,0:T(8,128)}, u32[]{:S(2)}, u32[]{:S(2)}) %all-to-all-start.1) | async-done | bytes 786464 | tf_op jit(solution)/shard_map/all_to_all | solution.py:45
  239.0 3.5 all-to-all-start.6
  243.7 9.7 %all-to-all-done.6 = f32[16,16,256]{2,1,0:T(8,128)S(1)} async-done(((f32[16,16,256]{2,1,0:T(8,128)}), f32[16,16,256]{2,1,0:T(8,128)S(1)}, u32[]{:S(2)}, u32[]{:S(2)}) %all-to-all-start.6) | async-done | bytes 262176 | tf_op jit(solution)/shard_map/all_to_all | solution.py:17
  254.3 4.5 %all-to-all-start.2 = ((f32[16,48,256]{2,1,0:T(8,128)}), f32[16,48,256]{2,1,0:T(8,128)}, u32[]{:S(2)}, u32[]{:S(2)}) async-start(f32[16,48,256]{2,1,0:T(8,128)} %broadcast_in_dim.26), calls=%async_computation.3 | async-start | bytes 1572864 | tf_op jit(solution)/shard_map/all_to_all | solution.py:17
  260.5 2.8 fusion.3
  263.3 16.2 %all-to-all-done.2 = f32[16,48,256]{2,1,0:T(8,128)} async-done(((f32[16,48,256]{2,1,0:T(8,128)}), f32[16,48,256]{2,1,0:T(8,128)}, u32[]{:S(2)}, u32[]{:S(2)}) %all-to-all-start.2) | async-done | bytes 786464 | tf_op jit(solution)/shard_map/all_to_all | solution.py:17
  284.5 2.4 subtract_subtract_fusion.1
  289.0 18.5 %all_to_all.67 = f32[16,48,256]{2,1,0:T(8,128)} all-to-all(f32[16,48,256]{2,1,0:T(8,128)S(1)} %fusion.39), channel_id=1, replica_groups=mesh['row'=16,'col'=16] {'col'}, dimensions={0} | all-to-all | bytes 1572864 | tf_op jit(solution)/shard_map/all_to_all | solution.py:45
  308.8 17.5 %all_to_all.68 = f32[16,48,256]{2,1,0:T(8,128)S(1)} all-to-all(f32[16,48,256]{2,1,0:T(8,128)S(1)} %broadcast_in_dim.30), channel_id=1, replica_groups=mesh['row'=16,'col'=16] {'col'}, dimensions={0} | all-to-all | bytes 1572864 | tf_op jit(solution)/shard_map/all_to_all | solution.py:17
  329.2 3.5 all-to-all-start.11
  332.7 5.9 %fusion.11 = f32[768,256]{1,0:T(8,128)} fusion(f32[768,768]{1,0:T(8,128)S(1)} %subtract_subtract_fusion.1, f32[1536,256]{1,0:T(8,128)} %all-gather.2.cloned.1.call-done), kind=kOutput, calls=%fused_computation.20 | convolution fusion | flops 1811939328 | bytes 3932160 | tf_op jit(solution)/shard_map/dot_general | solution.py:61
  338.6 7.8 %all-to-all-done.11 = f32[16,16,256]{2,1,0:T(8,128)S(1)} async-done(((f32[16,16,256]{2,1,0:T(8,128)}), f32[16,16,256]{2,1,0:T(8,128)S(1)}, u32[]{:S(2)}, u32[]{:S(2)}) %all-to-all-start.11) | async-done | bytes 262176 | tf_op jit(solution)/shard_map/all_to_all | solution.py:45
  346.4 4.3 all-to-all-start.7
  350.7 22.9 %all-to-all-done.7 = f32[16,48,256]{2,1,0:T(8,128)} async-done(((f32[16,48,256]{2,1,0:T(8,128)}), f32[16,48,256]{2,1,0:T(8,128)}, u32[]{:S(2)}, u32[]{:S(2)}) %all-to-all-start.7) | async-done | bytes 786464 | tf_op jit(solution)/shard_map/all_to_all | solution.py:45
  374.3 3.5 all-to-all-start.12
  379.1 10.0 %all-to-all-done.12 = f32[16,16,256]{2,1,0:T(8,128)S(1)} async-done(((f32[16,16,256]{2,1,0:T(8,128)}), f32[16,16,256]{2,1,0:T(8,128)S(1)}, u32[]{:S(2)}, u32[]{:S(2)}) %all-to-all-start.12) | async-done | bytes 262176 | tf_op jit(solution)/shard_map/all_to_all | solution.py:17
  390.0 4.5 %all-to-all-start.8 = ((f32[16,48,256]{2,1,0:T(8,128)}), f32[16,48,256]{2,1,0:T(8,128)}, u32[]{:S(2)}, u32[]{:S(2)}) async-start(f32[16,48,256]{2,1,0:T(8,128)} %broadcast_in_dim.29), calls=%async_computation.9 | async-start | bytes 1572864 | tf_op jit(solution)/shard_map/all_to_all | solution.py:17
  396.2 3.1 fusion
  399.3 16.0 %all-to-all-done.8 = f32[16,48,256]{2,1,0:T(8,128)} async-done(((f32[16,48,256]{2,1,0:T(8,128)}), f32[16,48,256]{2,1,0:T(8,128)}, u32[]{:S(2)}, u32[]{:S(2)}) %all-to-all-start.8) | async-done | bytes 786464 | tf_op jit(solution)/shard_map/all_to_all | solution.py:17
  420.4 3.8 subtract_subtract_fusion
  (61 shorter events, 34.8 us)
Async XLA Ops:
  8.7 49.2 %all-to-all-start = ((f32[16,2,48,256]{3,2,1,0:T(8,128)}), f32[16,2,48,256]{3,2,1,0:T(8,128)S(1)}, u32[]{:S(2)}, u32[]{:S(2)}) async-start(f32[16,2,48,256]{3,2,1,0:T(8,128)} %broadcast_in_dim.24), calls=%async_computation | async-start | bytes 3145728 | tf_op jit(solution)/shard_map/all_to_all | solution.py:17
  18.3 114.6 %reduce-scatter.2.cloned.1.call-start = ((), (), s32[]{:S(2)}) async-start(), calls=%async_computation.14 | async-start | bytes 1671168 | tf_op jit(solution)/shard_map/reduce_scatter | solution.py:34
  59.3 129.1 %all-gather.2.cloned.1.call-start = ((), (), s32[]{:S(2)}) async-start(), calls=%async_computation.15 | async-start | bytes 1671168 | tf_op jit(solution)/shard_map/all_gather | solution.py:35
  133.0 2.0 copy-start.3
  133.2 148.3 %copy-start.5 = (f32[1,16,48,256]{3,2,1,0:T(8,128)}, f32[1,16,48,256]{3,2,1,0:T(8,128)S(1)}, u32[]{:S(2)}) copy-start(f32[1,16,48,256]{3,2,1,0:T(8,128)S(1)} %get-tuple-element.6) | copy-start | bytes 2359300
  137.0 36.3 %copy-start.8 = (f32[2,256,256]{2,1,0:T(8,128)S(1)}, f32[2,256,256]{2,1,0:T(8,128)}, u32[]{:S(2)}) copy-start(f32[2,256,256]{2,1,0:T(8,128)} %param.5) | copy-start | bytes 1572868
  188.3 10.7 %copy-start = (f32[1536,256]{1,0:T(8,128)S(1)}, f32[1536,256]{1,0:T(8,128)}, u32[]{:S(2)}) copy-start(f32[1536,256]{1,0:T(8,128)} %all-gather.2.cloned.1.call-done) | copy-start | bytes 4718596
  191.9 19.5 %all-to-all-start.5 = ((f32[16,16,256]{2,1,0:T(8,128)}), f32[16,16,256]{2,1,0:T(8,128)S(1)}, u32[]{:S(2)}, u32[]{:S(2)}) async-start(f32[16,16,256]{2,1,0:T(8,128)} %bitcast.10), calls=%async_computation.6 | async-start | bytes 524288 | tf_op jit(solution)/shard_map/all_to_all | solution.py:45
  211.4 26.8 %all-to-all-start.1 = ((f32[16,48,256]{2,1,0:T(8,128)}), f32[16,48,256]{2,1,0:T(8,128)}, u32[]{:S(2)}, u32[]{:S(2)}) async-start(f32[16,48,256]{2,1,0:T(8,128)} %bitcast.86), calls=%async_computation.2 | async-start | bytes 1572864 | tf_op jit(solution)/shard_map/all_to_all | solution.py:45
  239.0 14.4 %all-to-all-start.6 = ((f32[16,16,256]{2,1,0:T(8,128)}), f32[16,16,256]{2,1,0:T(8,128)S(1)}, u32[]{:S(2)}, u32[]{:S(2)}) async-start(f32[16,16,256]{2,1,0:T(8,128)} %broadcast_in_dim.28), calls=%async_computation.7 | async-start | bytes 524288 | tf_op jit(solution)/shard_map/all_to_all | solution.py:17
  253.4 5.5 %copy-start.13 = (f32[16,16,256]{2,1,0:T(8,128)}, f32[16,16,256]{2,1,0:T(8,128)S(1)}, u32[]{:S(2)}) copy-start(f32[16,16,256]{2,1,0:T(8,128)S(1)} %all-to-all-done.6) | copy-start | bytes 786436
  254.3 25.1 %all-to-all-start.2 = ((f32[16,48,256]{2,1,0:T(8,128)}), f32[16,48,256]{2,1,0:T(8,128)}, u32[]{:S(2)}, u32[]{:S(2)}) async-start(f32[16,48,256]{2,1,0:T(8,128)} %broadcast_in_dim.26), calls=%async_computation.3 | async-start | bytes 1572864 | tf_op jit(solution)/shard_map/all_to_all | solution.py:17
  282.3 2.2 copy-start.4
  282.3 2.2 copy-start.6
  282.3 2.2 copy-start.11
  308.7 17.6 %copy-start.9 = (f32[2,256,256]{2,1,0:T(8,128)S(1)}, f32[2,256,256]{2,1,0:T(8,128)}, u32[]{:S(2)}) copy-start(f32[2,256,256]{2,1,0:T(8,128)} %param.5) | copy-start | bytes 1572868
  308.7 18.3 %copy-start.1 = (f32[1536,256]{1,0:T(8,128)S(1)}, f32[1536,256]{1,0:T(8,128)}, u32[]{:S(2)}) copy-start(f32[1536,256]{1,0:T(8,128)} %all-gather.2.cloned.1.call-done) | copy-start | bytes 4718596
  327.1 2.1 copy-start.7
  329.2 17.2 %all-to-all-start.11 = ((f32[16,16,256]{2,1,0:T(8,128)}), f32[16,16,256]{2,1,0:T(8,128)S(1)}, u32[]{:S(2)}, u32[]{:S(2)}) async-start(f32[16,16,256]{2,1,0:T(8,128)} %bitcast.20), calls=%async_computation.12 | async-start | bytes 524288 | tf_op jit(solution)/shard_map/all_to_all | solution.py:45
  346.4 27.2 %all-to-all-start.7 = ((f32[16,48,256]{2,1,0:T(8,128)}), f32[16,48,256]{2,1,0:T(8,128)}, u32[]{:S(2)}, u32[]{:S(2)}) async-start(f32[16,48,256]{2,1,0:T(8,128)} %bitcast.87), calls=%async_computation.8 | async-start | bytes 1572864 | tf_op jit(solution)/shard_map/all_to_all | solution.py:45
  374.3 14.7 %all-to-all-start.12 = ((f32[16,16,256]{2,1,0:T(8,128)}), f32[16,16,256]{2,1,0:T(8,128)S(1)}, u32[]{:S(2)}, u32[]{:S(2)}) async-start(f32[16,16,256]{2,1,0:T(8,128)} %broadcast_in_dim.31), calls=%async_computation.13 | async-start | bytes 524288 | tf_op jit(solution)/shard_map/all_to_all | solution.py:17
  389.1 5.5 %copy-start.12 = (f32[16,16,256]{2,1,0:T(8,128)}, f32[16,16,256]{2,1,0:T(8,128)S(1)}, u32[]{:S(2)}) copy-start(f32[16,16,256]{2,1,0:T(8,128)S(1)} %all-to-all-done.12) | copy-start | bytes 786436
  390.0 25.3 %all-to-all-start.8 = ((f32[16,48,256]{2,1,0:T(8,128)}), f32[16,48,256]{2,1,0:T(8,128)}, u32[]{:S(2)}, u32[]{:S(2)}) async-start(f32[16,48,256]{2,1,0:T(8,128)} %broadcast_in_dim.29), calls=%async_computation.9 | async-start | bytes 1572864 | tf_op jit(solution)/shard_map/all_to_all | solution.py:17
  415.3 2.9 copy-start.2
  418.2 2.2 copy-start.10
Sparse Core Ops, SparseCore 0:
  59.4 73.4 reduce-scatter.1
  135.6 52.7 all-gather.1
where the time goes:
time: 433 us; the launch traced here: 431 us
  waiting for transfers between devices  237 us (55%)
  blocking collectives  72.1 us (17%)
  matrix products  48.2 us (11%)
  starting transfers between devices  45 us (10%)
  between operations  13.8 us (3%)
  local copies, waits for them, and re-layouts  10.1 us (2%)
  other arithmetic  4.93 us (1%)
    all_to_all x5, waiting for transfers between devices, from_everyone(): return lax.all_to_all(copies, axis, split_axis=0, concat_axis=0, tiled=True)  91.4 us
    reduce_scatter x1, waiting for transfers between devices, broadcast_by_parts(): own = lax.psum_scatter(padded, axis, scatter_dimension=0, tiled=True)  73.6 us
    all_to_all x4, waiting for transfers between devices, sent_and_summed(): lax.all_to_all(tiles, axis, split_axis=0, concat_axis=0, tiled=True)  58.5 us
    all_to_all x2, blocking collectives, sent_and_summed(): lax.all_to_all(tiles, axis, split_axis=0, concat_axis=0, tiled=True)  37 us
    all_to_all x2, blocking collectives, from_everyone(): return lax.all_to_all(copies, axis, split_axis=0, concat_axis=0, tiled=True)  35.2 us
    all_to_all x5, starting transfers between devices, from_everyone(): return lax.all_to_all(copies, axis, split_axis=0, concat_axis=0, tiled=True)  25.7 us
    dot_general x6, matrix products, transposed_product(): lax.dot_general(left, right, (((0,), (0,)), ((), ())), precision=highest,...  19.5 us
    all_to_all x4, starting transfers between devices, sent_and_summed(): lax.all_to_all(tiles, axis, split_axis=0, concat_axis=0, tiled=True)  19.2 us
  transfers between devices with their start and end apart: 11, of which 11 were waited for; matrix products, arithmetic and copies ran while one was open for 7% of the time, Pallas kernels for 0%

commit v1 on v0

--- a/solution.py
+++ b/solution.py
@@ -4,6 +4,11 @@
 from jax.sharding import PartitionSpec as P
 
 highest = lax.Precision.HIGHEST
+
+
+def swapped_in(x, mesh_axis, d):
+    outgoing = jnp.stack([x] * lax.axis_size(mesh_axis))
+    return jnp.concatenate(lax.all_to_all(outgoing, mesh_axis, 0, 0), axis=d)
 
 
 def laid_out(tiles, dim):
@@ -32,7 +37,7 @@
     )
     padded = padded_to(lines, lax.axis_size(axis))
     own = lax.psum_scatter(padded, axis, scatter_dimension=0, tiled=True)
-    return lax.all_gather(own, axis, axis=0, tiled=True)[: len(lines)].reshape(value.shape)
+    return swapped_in(own, axis, 0)[: len(lines)].reshape(value.shape)
 
 
 def cut_along(value, dim, peers):

time: 433 us -> 414 us (0.956)
  waiting for transfers between devices: 237 us -> 207 us
  local copies, waits for them, and re-layouts: 10.1 us -> 21.9 us
  starting transfers between devices: 45 us -> 56.7 us
  blocking collectives: 72.1 us -> 62.1 us
    reduce_scatter x1, waiting for transfers between devices: 73.6 us -> 29.8 us  [broadcast_by_parts(): own = lax.psum_scatter(padded, axis, scatter_dimension=0, tiled=True)]
    all_to_all x0 -> x1, waiting for transfers between devices: none -> 19 us  [swapped_in(): return jnp.concatenate(lax.all_to_all(outgoing, mesh_axis, 0, 0), axis=d)]
    all_to_all x2 -> x1, blocking collectives: 35.2 us -> 19.3 us  [from_everyone(): return lax.all_to_all(copies, axis, split_axis=0, concat_axis=0, tiled=True)]
    all_gather x1 -> x0, waiting for transfers between devices: 13.4 us -> none  [broadcast_by_parts(): lax.all_gather(own, axis, axis=0, tiled=True)[:len(lines)]]
    all_to_all x5 -> x6, waiting for transfers between devices: 91.4 us -> 103 us  [from_everyone(): return lax.all_to_all(copies, axis, split_axis=0, concat_axis=0, tiled=True)]
    all_to_all x5 -> x6, starting transfers between devices: 25.7 us -> 31.9 us  [from_everyone(): return lax.all_to_all(copies, axis, split_axis=0, concat_axis=0, tiled=True)]
    all_to_all x2, blocking collectives: 37 us -> 42.8 us  [sent_and_summed(): lax.all_to_all(tiles, axis, split_axis=0, concat_axis=0, tiled=True)]
    dot_general x1 -> x4, local copies, waits for them, and re-layouts: 2.29 us -> 7.68 us  [transposed_product(): lax.dot_general(left, right, (((0,), (0,)), ((), ())), precision=highest,...]
  transfers between devices with their start and end apart: 11 -> 12, of which waited for: 11 -> 12; matrix products, arithmetic and copies ran while one was open for 7% -> 7% of each run, Pallas kernels for 0% -> 0%
where the time goes in v1:
time: 414 us; the launch traced here: 413 us
  waiting for transfers between devices  207 us (50%)
  blocking collectives  62.1 us (15%)
  starting transfers between devices  56.7 us (14%)
  matrix products  45.1 us (11%)
  local copies, waits for them, and re-layouts  21.9 us (5%)
  between operations  13.8 us (3%)
  other arithmetic  6.06 us (1%)
    all_to_all x6, waiting for transfers between devices, from_everyone(): return lax.all_to_all(copies, axis, split_axis=0, concat_axis=0, tiled=True)  103 us
    all_to_all x4, waiting for transfers between devices, sent_and_summed(): lax.all_to_all(tiles, axis, split_axis=0, concat_axis=0, tiled=True)  54.8 us
    all_to_all x2, blocking collectives, sent_and_summed(): lax.all_to_all(tiles, axis, split_axis=0, concat_axis=0, tiled=True)  42.8 us
    all_to_all x6, starting transfers between devices, from_everyone(): return lax.all_to_all(copies, axis, split_axis=0, concat_axis=0, tiled=True)  31.9 us
    reduce_scatter x1, waiting for transfers between devices, broadcast_by_parts(): own = lax.psum_scatter(padded, axis, scatter_dimension=0, tiled=True)  29.8 us
    all_to_all x4, starting transfers between devices, sent_and_summed(): lax.all_to_all(tiles, axis, split_axis=0, concat_axis=0, tiled=True)  19.3 us
    all_to_all x1, blocking collectives, from_everyone(): return lax.all_to_all(copies, axis, split_axis=0, concat_axis=0, tiled=True)  19.3 us
    dot_general x10, matrix products, matmul(): jnp.dot(left, right, precision=highest, preferred_element_type=jnp.float32)  19.1 us
  transfers between devices with their start and end apart: 12, of which 12 were waited for; matrix products, arithmetic and copies ran while one was open for 7% of the time, Pallas kernels for 0%

profile of v1, /device:TPU:2, one launch (start us, length us, event | category | flops | bytes accessed | tf_op | source)
XLA Modules:
  0.0 412.7 jit_solution(9758662847050238990)
XLA Ops:
  8.7 9.6 %all-to-all-start = ((f32[16,2,48,256]{3,2,1,0:T(8,128)}), f32[16,2,48,256]{3,2,1,0:T(8,128)S(1)}, u32[]{:S(2)}, u32[]{:S(2)}) async-start(f32[16,2,48,256]{3,2,1,0:T(8,128)} %broadcast_in_dim.24), calls=%async_computation | async-start | bytes 3145728 | tf_op jit(solution)/shard_map/all_to_all | solution.py:22
  18.4 39.6 %all-to-all-done = f32[16,2,48,256]{3,2,1,0:T(8,128)S(1)} async-done(((f32[16,2,48,256]{3,2,1,0:T(8,128)}), f32[16,2,48,256]{3,2,1,0:T(8,128)S(1)}, u32[]{:S(2)}, u32[]{:S(2)}) %all-to-all-start) | async-done | bytes 1572896 | tf_op jit(solution)/shard_map/all_to_all | solution.py:22
  63.3 19.7 %all_to_all.70 = f32[16,48,256]{2,1,0:T(8,128)} all-to-all(f32[16,48,256]{2,1,0:T(8,128)S(1)} %fusion.30), channel_id=1, replica_groups=mesh['row'=16,'col'=16] {'col'}, dimensions={0} | all-to-all | bytes 1572864 | tf_op jit(solution)/shard_map/all_to_all | solution.py:50
  84.3 19.3 %all_to_all.71 = f32[16,48,256]{2,1,0:T(8,128)} all-to-all(f32[16,48,256]{2,1,0:T(8,128)S(1)} %broadcast_in_dim.27), channel_id=1, replica_groups=mesh['row'=16,'col'=16] {'col'}, dimensions={0} | all-to-all | bytes 1572864 | tf_op jit(solution)/shard_map/all_to_all | solution.py:22
  103.6 29.8 %reduce-scatter.2.cloned.1.call-done = f32[96,256]{1,0:T(8,128)} async-done(((f32[1536,256]{1,0:T(8,128)}), f32[96,256]{1,0:T(8,128)}) %reduce-scatter.2.cloned.1.call-update) | async-done | bytes 98320 | tf_op jit(solution)/shard_map/reduce_scatter | solution.py:39
  135.6 5.4 %all-to-all-start.1 = ((f32[16,96,256]{2,1,0:T(8,128)}), f32[16,96,256]{2,1,0:T(8,128)}, u32[]{:S(2)}, u32[]{:S(2)}) async-start(f32[16,96,256]{2,1,0:T(8,128)} %stack.2), calls=%async_computation.2 | async-start | bytes 3145728 | tf_op jit(solution)/shard_map/all_to_all | solution.py:11
  141.0 2.8 fusion.18
  143.8 19.0 %all-to-all-done.1 = f32[16,96,256]{2,1,0:T(8,128)} async-done(((f32[16,96,256]{2,1,0:T(8,128)}), f32[16,96,256]{2,1,0:T(8,128)}, u32[]{:S(2)}, u32[]{:S(2)}) %all-to-all-start.1) | async-done | bytes 1572896 | tf_op jit(solution)/shard_map/all_to_all | solution.py:11
  167.4 2.9 fusion.8
  170.3 7.2 %all-to-all-start.6 = ((f32[16,16,256]{2,1,0:T(8,128)}), f32[16,16,256]{2,1,0:T(8,128)S(1)}, u32[]{:S(2)}, u32[]{:S(2)}) async-start(f32[16,16,256]{2,1,0:T(8,128)} %fusion.8), calls=%async_computation.7 | async-start | bytes 524288 | tf_op jit(solution)/shard_map/all_to_all | solution.py:50
  177.6 4.2 %convolution_bitcast_fusion = f32[768,256]{0,1:T(8,128)} fusion(f32[768,256]{1,0:T(8,128)} %bitcast.103, f32[768,768]{1,0:T(8,128)S(1)} %copy-done), kind=kOutput, calls=%fused_computation.3 | convolution fusion | flops 1811939328 | bytes 3932160 | tf_op jit(solution)/shard_map/dot_general | solution.py:66
  184.0 5.1 %all-to-all-done.6 = f32[16,16,256]{2,1,0:T(8,128)S(1)} async-done(((f32[16,16,256]{2,1,0:T(8,128)}), f32[16,16,256]{2,1,0:T(8,128)S(1)}, u32[]{:S(2)}, u32[]{:S(2)}) %all-to-all-start.6) | async-done | bytes 262176 | tf_op jit(solution)/shard_map/all_to_all | solution.py:50
  189.1 4.3 %all-to-all-start.2 = ((f32[16,48,256]{2,1,0:T(8,128)}), f32[16,48,256]{2,1,0:T(8,128)}, u32[]{:S(2)}, u32[]{:S(2)}) async-start(f32[16,48,256]{2,1,0:T(8,128)} %bitcast.4), calls=%async_computation.3 | async-start | bytes 1572864 | tf_op jit(solution)/shard_map/all_to_all | solution.py:50
  193.5 21.1 %all-to-all-done.2 = f32[16,48,256]{2,1,0:T(8,128)} async-done(((f32[16,48,256]{2,1,0:T(8,128)}), f32[16,48,256]{2,1,0:T(8,128)}, u32[]{:S(2)}, u32[]{:S(2)}) %all-to-all-start.2) | async-done | bytes 786464 | tf_op jit(solution)/shard_map/all_to_all | solution.py:50
  215.4 3.5 all-to-all-start.7
  220.1 9.5 %all-to-all-done.7 = f32[16,16,256]{2,1,0:T(8,128)S(1)} async-done(((f32[16,16,256]{2,1,0:T(8,128)}), f32[16,16,256]{2,1,0:T(8,128)S(1)}, u32[]{:S(2)}, u32[]{:S(2)}) %all-to-all-start.7) | async-done | bytes 262176 | tf_op jit(solution)/shard_map/all_to_all | solution.py:22
  230.5 4.5 %all-to-all-start.3 = ((f32[16,48,256]{2,1,0:T(8,128)}), f32[16,48,256]{2,1,0:T(8,128)}, u32[]{:S(2)}, u32[]{:S(2)}) async-start(f32[16,48,256]{2,1,0:T(8,128)} %broadcast_in_dim.26), calls=%async_computation.4 | async-start | bytes 1572864 | tf_op jit(solution)/shard_map/all_to_all | solution.py:22
  237.3 17.3 %all-to-all-done.3 = f32[16,48,256]{2,1,0:T(8,128)} async-done(((f32[16,48,256]{2,1,0:T(8,128)}), f32[16,48,256]{2,1,0:T(8,128)}, u32[]{:S(2)}, u32[]{:S(2)}) %all-to-all-start.3) | async-done | bytes 786464 | tf_op jit(solution)/shard_map/all_to_all | solution.py:22
  264.2 23.1 %all_to_all.72 = f32[16,48,256]{2,1,0:T(8,128)} all-to-all(f32[16,48,256]{2,1,0:T(8,128)S(1)} %fusion.33), channel_id=1, replica_groups=mesh['row'=16,'col'=16] {'col'}, dimensions={0} | all-to-all | bytes 1572864 | tf_op jit(solution)/shard_map/all_to_all | solution.py:50
  289.4 6.3 %all-to-all-start.11 = ((f32[16,48,256]{2,1,0:T(8,128)}), f32[16,48,256]{2,1,0:T(8,128)}, u32[]{:S(2)}, u32[]{:S(2)}) async-start(f32[16,48,256]{2,1,0:T(8,128)} %broadcast_in_dim.30), calls=%async_computation.12 | async-start | bytes 1572864 | tf_op jit(solution)/shard_map/all_to_all | solution.py:22
  296.8 11.7 %all-to-all-done.11 = f32[16,48,256]{2,1,0:T(8,128)} async-done(((f32[16,48,256]{2,1,0:T(8,128)}), f32[16,48,256]{2,1,0:T(8,128)}, u32[]{:S(2)}, u32[]{:S(2)}) %all-to-all-start.11) | async-done | bytes 786464 | tf_op jit(solution)/shard_map/all_to_all | solution.py:22
  313.0 3.5 all-to-all-start.12
  318.5 4.6 %fusion.32 = f32[16,48,256]{2,1,0:T(8,128)} fusion(f32[16,48,768]{2,1,0:T(8,128)} %bitcast.112, f32[768,256,1]{1,0,2:T(8,128)S(1)} %bitcast.99), kind=kOutput, calls=%fused_computation.41 | convolution fusion | flops 1811939328 | bytes 3932160 | tf_op jit(solution)/shard_map/dot_general | solution.py:66
  323.0 6.4 %all-to-all-done.12 = f32[16,16,256]{2,1,0:T(8,128)S(1)} async-done(((f32[16,16,256]{2,1,0:T(8,128)}), f32[16,16,256]{2,1,0:T(8,128)S(1)}, u32[]{:S(2)}, u32[]{:S(2)}) %all-to-all-start.12) | async-done | bytes 262176 | tf_op jit(solution)/shard_map/all_to_all | solution.py:50
  329.5 4.3 %all-to-all-start.8 = ((f32[16,48,256]{2,1,0:T(8,128)}), f32[16,48,256]{2,1,0:T(8,128)}, u32[]{:S(2)}, u32[]{:S(2)}) async-start(f32[16,48,256]{2,1,0:T(8,128)} %fusion.32), calls=%async_computation.9 | async-start | bytes 1572864 | tf_op jit(solution)/shard_map/all_to_all | solution.py:50
  333.8 22.1 %all-to-all-done.8 = f32[16,48,256]{2,1,0:T(8,128)} async-done(((f32[16,48,256]{2,1,0:T(8,128)}), f32[16,48,256]{2,1,0:T(8,128)}, u32[]{:S(2)}, u32[]{:S(2)}) %all-to-all-start.8) | async-done | bytes 786464 | tf_op jit(solution)/shard_map/all_to_all | solution.py:50
  356.6 3.5 all-to-all-start.13
  361.4 9.9 %all-to-all-done.13 = f32[16,16,256]{2,1,0:T(8,128)S(1)} async-done(((f32[16,16,256]{2,1,0:T(8,128)}), f32[16,16,256]{2,1,0:T(8,128)S(1)}, u32[]{:S(2)}, u32[]{:S(2)}) %all-to-all-start.13) | async-done | bytes 262176 | tf_op jit(solution)/shard_map/all_to_all | solution.py:22
  372.2 4.5 %all-to-all-start.9 = ((f32[16,48,256]{2,1,0:T(8,128)}), f32[16,48,256]{2,1,0:T(8,128)}, u32[]{:S(2)}, u32[]{:S(2)}) async-start(f32[16,48,256]{2,1,0:T(8,128)} %broadcast_in_dim.29), calls=%async_computation.10 | async-start | bytes 1572864 | tf_op jit(solution)/shard_map/all_to_all | solution.py:22
  378.4 2.8 fusion
  381.2 15.7 %all-to-all-done.9 = f32[16,48,256]{2,1,0:T(8,128)} async-done(((f32[16,48,256]{2,1,0:T(8,128)}), f32[16,48,256]{2,1,0:T(8,128)}, u32[]{:S(2)}, u32[]{:S(2)}) %all-to-all-start.9) | async-done | bytes 786464 | tf_op jit(solution)/shard_map/all_to_all | solution.py:22
  402.0 3.8 subtract_subtract_fusion
  (70 shorter events, 52.0 us)
Async XLA Ops:
  8.7 49.2 %all-to-all-start = ((f32[16,2,48,256]{3,2,1,0:T(8,128)}), f32[16,2,48,256]{3,2,1,0:T(8,128)S(1)}, u32[]{:S(2)}, u32[]{:S(2)}) async-start(f32[16,2,48,256]{3,2,1,0:T(8,128)} %broadcast_in_dim.24), calls=%async_computation | async-start | bytes 3145728 | tf_op jit(solution)/shard_map/all_to_all | solution.py:22
  18.3 115.1 %reduce-scatter.2.cloned.1.call-start = ((), (), s32[]{:S(2)}) async-start(), calls=%async_computation.15 | async-start | bytes 1671168 | tf_op jit(solution)/shard_map/reduce_scatter | solution.py:39
  59.4 2.0 copy-start
  60.4 22.7 %copy-start.5 = (f32[1,16,48,256]{3,2,1,0:T(8,128)}, f32[1,16,48,256]{3,2,1,0:T(8,128)S(1)}, u32[]{:S(2)}) copy-start(f32[1,16,48,256]{3,2,1,0:T(8,128)S(1)} %get-tuple-element.6) | copy-start | bytes 2359300
  103.6 37.4 %copy-start.10 = (f32[2,256,256]{2,1,0:T(8,128)S(1)}, f32[2,256,256]{2,1,0:T(8,128)}, u32[]{:S(2)}) copy-start(f32[2,256,256]{2,1,0:T(8,128)} %param.5) | copy-start | bytes 1572868
  135.6 27.1 %all-to-all-start.1 = ((f32[16,96,256]{2,1,0:T(8,128)}), f32[16,96,256]{2,1,0:T(8,128)}, u32[]{:S(2)}, u32[]{:S(2)}) async-start(f32[16,96,256]{2,1,0:T(8,128)} %stack.2), calls=%async_computation.2 | async-start | bytes 3145728 | tf_op jit(solution)/shard_map/all_to_all | solution.py:11
  170.3 18.8 %all-to-all-start.6 = ((f32[16,16,256]{2,1,0:T(8,128)}), f32[16,16,256]{2,1,0:T(8,128)S(1)}, u32[]{:S(2)}, u32[]{:S(2)}) async-start(f32[16,16,256]{2,1,0:T(8,128)} %fusion.8), calls=%async_computation.7 | async-start | bytes 524288 | tf_op jit(solution)/shard_map/all_to_all | solution.py:50
  189.1 25.5 %all-to-all-start.2 = ((f32[16,48,256]{2,1,0:T(8,128)}), f32[16,48,256]{2,1,0:T(8,128)}, u32[]{:S(2)}, u32[]{:S(2)}) async-start(f32[16,48,256]{2,1,0:T(8,128)} %bitcast.4), calls=%async_computation.3 | async-start | bytes 1572864 | tf_op jit(solution)/shard_map/all_to_all | solution.py:50
  193.4 41.6 %copy-start.11 = (f32[2,256,256]{2,1,0:T(8,128)S(1)}, f32[2,256,256]{2,1,0:T(8,128)}, u32[]{:S(2)}) copy-start(f32[2,256,256]{2,1,0:T(8,128)} %param.5) | copy-start | bytes 1572868
  193.5 42.1 %copy-start.2 = (f32[8,96,256]{2,1,0:T(8,128)S(1)}, f32[8,96,256]{2,1,0:T(8,128)}, u32[]{:S(2)}) copy-start(f32[8,96,256]{2,1,0:T(8,128)} %get-tuple-element.8) | copy-start | bytes 2359300
  193.5 42.1 %copy-start.8 = (f32[768,256]{1,0:T(8,128)S(1)}, f32[768,256]{1,0:T(8,128)}, u32[]{:S(2)}) copy-start(f32[768,256]{1,0:T(8,128)} %fusion.18) | copy-start | bytes 2359300
  215.4 14.2 %all-to-all-start.7 = ((f32[16,16,256]{2,1,0:T(8,128)}), f32[16,16,256]{2,1,0:T(8,128)S(1)}, u32[]{:S(2)}, u32[]{:S(2)}) async-start(f32[16,16,256]{2,1,0:T(8,128)} %broadcast_in_dim.28), calls=%async_computation.8 | async-start | bytes 524288 | tf_op jit(solution)/shard_map/all_to_all | solution.py:22
  230.5 24.1 %all-to-all-start.3 = ((f32[16,48,256]{2,1,0:T(8,128)}), f32[16,48,256]{2,1,0:T(8,128)}, u32[]{:S(2)}, u32[]{:S(2)}) async-start(f32[16,48,256]{2,1,0:T(8,128)} %broadcast_in_dim.26), calls=%async_computation.4 | async-start | bytes 1572864 | tf_op jit(solution)/shard_map/all_to_all | solution.py:22
  235.6 21.0 %copy-start.6 = (f32[1,16,48,256]{3,2,1,0:T(8,128)S(1)}, f32[1,16,48,256]{3,2,1,0:T(8,128)}, u32[]{:S(2)}) copy-start(f32[1,16,48,256]{3,2,1,0:T(8,128)} %copy-done.5) | copy-start | bytes 2359300
  257.4 2.2 copy-start.1
  257.5 2.2 copy-start.7
  257.5 2.2 copy-start.14
  259.7 2.4 copy-start.3
  289.4 19.1 %all-to-all-start.11 = ((f32[16,48,256]{2,1,0:T(8,128)}), f32[16,48,256]{2,1,0:T(8,128)}, u32[]{:S(2)}, u32[]{:S(2)}) async-start(f32[16,48,256]{2,1,0:T(8,128)} %broadcast_in_dim.30), calls=%async_computation.12 | async-start | bytes 1572864 | tf_op jit(solution)/shard_map/all_to_all | solution.py:22
  308.5 2.9 copy-start.12
  310.6 0.9 copy-start.9
  313.0 16.5 %all-to-all-start.12 = ((f32[16,16,256]{2,1,0:T(8,128)}), f32[16,16,256]{2,1,0:T(8,128)S(1)}, u32[]{:S(2)}, u32[]{:S(2)}) async-start(f32[16,16,256]{2,1,0:T(8,128)} %fusion.6), calls=%async_computation.13 | async-start | bytes 524288 | tf_op jit(solution)/shard_map/all_to_all | solution.py:50
  329.5 26.4 %all-to-all-start.8 = ((f32[16,48,256]{2,1,0:T(8,128)}), f32[16,48,256]{2,1,0:T(8,128)}, u32[]{:S(2)}, u32[]{:S(2)}) async-start(f32[16,48,256]{2,1,0:T(8,128)} %fusion.32), calls=%async_computation.9 | async-start | bytes 1572864 | tf_op jit(solution)/shard_map/all_to_all | solution.py:50
  356.6 14.6 %all-to-all-start.13 = ((f32[16,16,256]{2,1,0:T(8,128)}), f32[16,16,256]{2,1,0:T(8,128)S(1)}, u32[]{:S(2)}, u32[]{:S(2)}) async-start(f32[16,16,256]{2,1,0:T(8,128)} %broadcast_in_dim.31), calls=%async_computation.14 | async-start | bytes 524288 | tf_op jit(solution)/shard_map/all_to_all | solution.py:22
  371.2 5.5 %copy-start.15 = (f32[16,16,256]{2,1,0:T(8,128)}, f32[16,16,256]{2,1,0:T(8,128)S(1)}, u32[]{:S(2)}) copy-start(f32[16,16,256]{2,1,0:T(8,128)S(1)} %all-to-all-done.13) | copy-start | bytes 786436
  372.2 24.7 %all-to-all-start.9 = ((f32[16,48,256]{2,1,0:T(8,128)}), f32[16,48,256]{2,1,0:T(8,128)}, u32[]{:S(2)}, u32[]{:S(2)}) async-start(f32[16,48,256]{2,1,0:T(8,128)} %broadcast_in_dim.29), calls=%async_computation.10 | async-start | bytes 1572864 | tf_op jit(solution)/shard_map/all_to_all | solution.py:22
  396.9 2.1 copy-start.4
  399.8 2.2 copy-start.13
Sparse Core Ops, SparseCore 0:
  59.4 74.0 reduce-scatter.1
